TPU v7x, 32 devices: a whole 2x2x4 slice. The times are simulated.
32 devices in a mesh: col: 8 (over y, x, core), grp: 4 (over z).
Axes of the slice: x: 2, y: 2, z: 4, core: 2. Of those that a mesh axis runs over, the one named last changes fastest.
Arguments:
- profiles: float32 [2048, 116], P('col'), may hold values from -6 to 6
- courant: float32 [2048, 58], P('col'), may hold values from -0.7 to 0.7
- owner_map: int32 [2048], replicated, may hold values from 0 to 2047, as said below
- cloud_flags: int32 [2048], P('col'), may hold values 0 or 1
- crm_state: float32 [2, 58, 64, 2048], P(None, None, 'grp', 'col'), may hold values from -6 to 6
Outputs:
- tendency: float32 [2048, 116], P('col')
- crm_final: float32 [2, 58, 64, 2048], P(None, None, 'grp', 'col')
Inputs may be any that keep to these rules, and one draw needn't show every extreme that they name: owner_map is a permutation; physics column p lives in span p // 256, element column e in group e // 256; each group hands at most 34 columns to one span, and exactly 34 to some spans, and every span receives exactly 256 columns.
All inputs are finite; a program needn't handle non-finite values. No bound on the sum of `cloud_flags` on one device may be relied on, other than what follows from the above.
Results may differ from a plain program's by a relative error of at most 0.00002.
Values sent between devices are 32-bit elements; how exact they have to be, the bound alone decides.
A program may use at most 64 MiB of HBM per device.

v0:
```python
import jax
import jax.numpy as jnp
from jax import lax
from jax.sharding import PartitionSpec as P

STEPS = 8


diffuse_x = 0.25
diffuse_z = 0.2
sat_scale = 0.5
sat_slope = 0.3
cond_rate = 0.5
latent_gain = 0.4


def padded(x, sides, width):
    for axis, dim in sides:
        peers, length = (lax.axis_size(axis), x.shape[dim])
        up = [(i, (i + 1) % peers) for i in range(peers)]
        down = [(j, i) for i, j in up]
        last = lax.slice_in_dim(x, length - width, length, axis=dim)
        leading = lax.slice_in_dim(x, 0, width, axis=dim)
        before = lax.ppermute(last, axis, up)
        after = lax.ppermute(leading, axis, down)
        x = jnp.concatenate([before, x, after], axis=dim)
    return x


def condense(fields, cloudy):
    energy = fields[0]
    moisture = fields[1]
    saturation = sat_scale * (jnp.exp(sat_slope * energy) - 1.0)
    amount = cond_rate * jnp.maximum(moisture - saturation, 0.0) * cloudy
    return jnp.stack([energy + latent_gain * amount, moisture - amount])


def advance(widened, courant_here, forcing, cloudy):
    centre = widened[:, :, 1:-1]
    eastern = widened[:, :, 2:]
    western = widened[:, :, :-2]
    upper = jnp.concatenate([centre[:, 1:], centre[:, -1:]], axis=1)
    lower = jnp.concatenate([centre[:, :1], centre[:, :-1]], axis=1)
    stepped = (
        centre
        + courant_here * ((western - eastern) * 0.5)
        + diffuse_x * (eastern - 2.0 * centre + western)
        + diffuse_z * (upper - 2.0 * centre + lower)
        + forcing
    )
    return condense(stepped, cloudy)


def on_device(profiles, courant, owner_map, cloud_flags, crm_state):
    columns = profiles.shape[0]
    levels = courant.shape[1]
    col_count = lax.axis_size("col")
    col_index = lax.axis_index("col")
    per_peer = columns // col_count
    capacity = per_peer + min(2, per_peer)
    positions = jnp.arange(columns, dtype=jnp.int32)
    my_owner = lax.dynamic_slice_in_dim(owner_map, col_index * columns, columns)
    target = my_owner // columns
    earlier = (target[:, None] == target[None, :]) & (positions[None, :] < positions[:, None])
    order_in = jnp.sum(earlier.astype(jnp.int32), axis=1)
    sent_slot = target * capacity + order_in
    send_rows = jnp.full((col_count * capacity,), columns, jnp.int32).at[sent_slot].set(positions)
    padded_prof = jnp.concatenate([profiles, jnp.zeros((1, profiles.shape[1]), jnp.float32)])
    padded_cour = jnp.concatenate([courant, jnp.zeros((1, levels), jnp.float32)])
    out_prof = padded_prof[send_rows].reshape(col_count, capacity, profiles.shape[1])
    out_cour = padded_cour[send_rows].reshape(col_count, capacity, levels)
    got_prof, got_cour = (
        lax.all_to_all(out_prof, "col", split_axis=0, concat_axis=0, tiled=True),
        lax.all_to_all(out_cour, "col", split_axis=0, concat_axis=0, tiled=True),
    )
    block_view = owner_map.reshape(col_count, columns)
    landing = (block_view // columns == col_index).astype(jnp.int32)
    before = jnp.cumsum(landing, axis=1) - landing
    sources = jnp.arange(col_count, dtype=jnp.int32)[:, None]
    where_from = sources * capacity + before
    landing_slot = jnp.where(landing > 0, block_view - col_index * columns, columns)
    senders_block = 4
    slot_blocks = landing_slot.reshape(col_count // senders_block, senders_block * columns)
    from_blocks = where_from.reshape(col_count // senders_block, senders_block * columns)

    def match_block(found, pair):
        slots, anchors = pair
        hits = slots[None, :] == positions[:, None]
        return (found + jnp.sum(jnp.where(hits, anchors[None, :], 0), axis=1), None)

    take_rows, unused = lax.scan(
        match_block, jnp.zeros((columns,), jnp.int32), (slot_blocks, from_blocks)
    )
    phys_prof = got_prof.reshape(col_count * capacity, profiles.shape[1])[take_rows]
    phys_cour = got_cour.reshape(col_count * capacity, levels)[take_rows]
    forcing = (phys_prof.reshape(columns, 2, levels).transpose(1, 2, 0) / STEPS)[:, :, None, :]
    courant_here = phys_cour.T[None, :, None, :]
    cloudy = cloud_flags.astype(jnp.float32)
    crm_now = crm_state
    for repeat in range(STEPS // 2):
        widened = padded(crm_now, (("grp", 2),), 2)
        middle = advance(widened, courant_here, forcing, cloudy)
        crm_now = advance(middle, courant_here, forcing, cloudy)
    cells_all = crm_state.shape[2] * lax.axis_size("grp")
    partial_value = jnp.sum(crm_now, axis=2) - jnp.sum(crm_state, axis=2)
    totals = lax.psum(partial_value, "grp")
    increment = totals / cells_all
    phys_inc = increment.transpose(2, 0, 1).reshape(columns, 2 * levels)
    back_rows = (
        jnp.zeros((col_count * capacity, 2 * levels), jnp.float32).at[take_rows].set(phys_inc)
    )
    got_back = lax.all_to_all(
        back_rows.reshape(col_count, capacity, 2 * levels),
        "col",
        split_axis=0,
        concat_axis=0,
        tiled=True,
    )
    tendency = got_back.reshape(col_count * capacity, 2 * levels)[sent_slot]
    return (tendency, crm_now)


def solution(mesh):
    placed = (P("col", None), P("col", None), P(), P("col"), P(None, None, "grp", "col"))
    return jax.shard_map(
        on_device,
        mesh=mesh,
        in_specs=placed,
        out_specs=(P("col", None), P(None, None, "grp", "col")),
        check_vma=False,
    )
```

profile of v0, /device:TPU:0, one launch (start us, length us, event | category | flops | bytes accessed | tf_op | source)
XLA Modules:
  0.0 158.9 jit_solution(1841023109057067718)
XLA Ops:
  7.2 0.9 and_select_fusion.1
  8.3 0.8 compare_select_fusion.2
  9.1 1.4 scatter_custom_fusion
  10.5 0.9 copy.71
  11.5 1.1 gather_fusion
  12.6 0.9 reshape.148
  13.4 5.2 %all-to-all-start = ((f32[8,1,1972]{2,1,0:T(1,128)}), f32[8,1,1972]{2,1,0:T(1,128)S(1)}, u32[]{:S(2)}, u32[]{:S(2)}) async-start(f32[8,1,1972]{2,1,0:T(1,128)} %reshape.148), calls=%async_computation | async-start | bytes 131072 | tf_op jit(solution)/shard_map/all_to_all | solution.py:74
  18.8 1.6 %collective-permute-start = (f32[2,58,2,256]{3,1,2,0:T(8,128)S(1)}, f32[2,58,2,256]{3,1,2,0:T(8,128)S(1)}, u32[]{:S(2)}, u32[]{:S(2)}) collective-permute-start(f32[2,58,2,256]{3,1,2,0:T(8,128)S(1)} %copy.84), channel_id=1, source_target_pairs={{0,1},{1,2},{2,3},{3,0},{4,5},{5,6},{6,7},{7,4},{8,9},{9,10},{10,1... | collective-permute-start | bytes 712712 | tf_op jit(solution)/shard_map/ppermute | solution.py:24
  20.5 2.3 %collective-permute-start.1 = (f32[2,58,2,256]{3,1,2,0:T(8,128)S(1)}, f32[2,58,2,256]{3,1,2,0:T(8,128)S(1)}, u32[]{:S(2)}, u32[]{:S(2)}) collective-permute-start(f32[2,58,2,256]{3,1,2,0:T(8,128)S(1)} %copy.85), channel_id=1, source_target_pairs={{1,0},{2,1},{3,2},{0,3},{5,4},{6,5},{7,6},{4,7},{9,8},{10,9},{11,1... | collective-permute-start | bytes 712712 | tf_op jit(solution)/shard_map/ppermute | solution.py:25
  24.6 1.1 gather_fusion.2
  25.6 0.7 reshape.75
  26.3 4.2 %all-to-all-start.1 = ((f32[8,34,116]{2,1,0:T(8,128)}), f32[8,34,116]{2,1,0:T(8,128)S(1)}, u32[]{:S(2)}, u32[]{:S(2)}) async-start(f32[8,34,116]{2,1,0:T(8,128)} %reshape.75), calls=%async_computation.1 | async-start | bytes 327680 | tf_op jit(solution)/shard_map/all_to_all | solution.py:73
  31.1 0.8 reduce.2
  32.0 0.7 gather_fusion.1
  32.9 3.5 %all-to-all-done.1 = f32[8,34,116]{2,1,0:T(8,128)S(1)} async-done(((f32[8,34,116]{2,1,0:T(8,128)}), f32[8,34,116]{2,1,0:T(8,128)S(1)}, u32[]{:S(2)}, u32[]{:S(2)}) %all-to-all-start.1) | async-done | bytes 126240 | tf_op jit(solution)/shard_map/all_to_all | solution.py:73
  36.4 0.7 gather_fusion.3
  37.3 1.3 constant_dynamic-update-slice_fusion.6
  39.4 1.8 %fusion.44 = f32[2,58,18,256]{3,1,2,0:T(8,128)S(1)} fusion(f32[2,1,18,256]{3,1,2,0:T(1,128)S(1)} %get-tuple-element.78, f32[2,57,18,256]{3,1,2,0:T(8,128)S(1)} %get-tuple-element.80, f32[2,57,18,256]{3,1,2,0:T(8,128)S(1)} %get-tuple-element.79, f32[2,1,18,256]{3,1,2,0:T(1,128)S(1)} %get-tuple-element.77, f32[2,58,18,256]{3,1,2,0:T(8,128)S(1)} %get-tuple-element.115, ...), kind=kLoop, calls=%fused_computation.133 | loop fusion | flops 8017920 | bytes 13006848 | tf_op jit(solution)/shard_map/add | solution.py:45
  42.0 1.7 %fusion.80 = f32[2,58,16,256]{3,1,2,0:T(8,128)S(1)} fusion(f32[1,58,18,256]{3,1,2,0:T(8,128)S(1)} %get-tuple-element.88, f32[1,58,18,256]{3,1,2,0:T(8,128)S(1)} %get-tuple-element.87, f32[2,1,16,256]{3,1,2,0:T(1,128)S(1)} %get-tuple-element.96, f32[2,57,16,256]{3,1,2,0:T(8,128)S(1)} %fusion.60, f32[2,1,16,256]{3,1,2,0:T(1,128)S(1)} %get-tuple-element.95, ...), kind=kLoop, calls=%fused_computation.179 | loop fusion | flops 9027584 | bytes 6150144 | tf_op jit(solution)/shard_map/add | solution.py:45
  44.3 3.8 %collective-permute-start.3 = (f32[2,58,2,256]{3,1,2,0:T(8,128)S(1)}, f32[2,58,2,256]{3,1,2,0:T(8,128)S(1)}, u32[]{:S(2)}, u32[]{:S(2)}) collective-permute-start(f32[2,58,2,256]{3,1,2,0:T(8,128)S(1)} %get-tuple-element.111), channel_id=1, source_target_pairs={{1,0},{2,1},{3,2},{0,3},{5,4},{6,5},{7,6},{4,7},{9,8},{10,9},{11,1... | collective-permute-start | bytes 712712 | tf_op jit(solution)/shard_map/ppermute | solution.py:25
  48.1 7.2 %collective-permute-done.2 = f32[2,58,2,256]{3,1,2,0:T(8,128)S(1)} collective-permute-done((f32[2,58,2,256]{3,1,2,0:T(8,128)S(1)}, f32[2,58,2,256]{3,1,2,0:T(8,128)S(1)}, u32[]{:S(2)}, u32[]{:S(2)}) %collective-permute-start.2) | collective-permute-done | bytes 237600 | tf_op jit(solution)/shard_map/ppermute | solution.py:24
  55.2 2.6 %collective-permute-done.3 = f32[2,58,2,256]{3,1,2,0:T(8,128)S(1)} collective-permute-done((f32[2,58,2,256]{3,1,2,0:T(8,128)S(1)}, f32[2,58,2,256]{3,1,2,0:T(8,128)S(1)}, u32[]{:S(2)}, u32[]{:S(2)}) %collective-permute-start.3) | collective-permute-done | bytes 237600 | tf_op jit(solution)/shard_map/ppermute | solution.py:25
  58.1 0.6 fusion.109
  58.8 2.2 %fusion.10 = f32[2,58,18,256]{3,1,2,0:T(8,128)S(1)} fusion(f32[1,58,16,256]{3,1,2,0:T(8,128)S(1)} %get-tuple-element.104, f32[1,58,16,256]{3,1,2,0:T(8,128)S(1)} %get-tuple-element.103, f32[2,58,2,256]{3,1,2,0:T(8,128)S(1)} %collective-permute-done.2, f32[2,58,2,256]{3,1,2,0:T(8,128)S(1)} %collective-permute-done.3, ...), kind=kLoop, calls=%fused_computation.96 | loop fusion | flops 18708480 | bytes 11032576 | tf_op jit(solution)/shard_map/add | solution.py:45
  61.7 1.7 %fusion.75 = f32[2,58,16,256]{3,1,2,0:T(8,128)S(1)} fusion(f32[1,58,18,256]{3,1,2,0:T(8,128)S(1)} %get-tuple-element.86, f32[1,58,18,256]{3,1,2,0:T(8,128)S(1)} %get-tuple-element.85, f32[2,1,16,256]{3,1,2,0:T(1,128)S(1)} %get-tuple-element.94, f32[2,57,16,256]{3,1,2,0:T(8,128)S(1)} %fusion.56, f32[2,1,16,256]{3,1,2,0:T(1,128)S(1)} %get-tuple-element.93, ...), kind=kLoop, calls=%fused_computation.173 | loop fusion | flops 9027584 | bytes 6150144 | tf_op jit(solution)/shard_map/add | solution.py:45
  63.9 0.9 collective-permute-start.4
  64.8 3.0 %collective-permute-start.5 = (f32[2,58,2,256]{3,1,2,0:T(8,128)S(1)}, f32[2,58,2,256]{3,1,2,0:T(8,128)S(1)}, u32[]{:S(2)}, u32[]{:S(2)}) collective-permute-start(f32[2,58,2,256]{3,1,2,0:T(8,128)S(1)} %get-tuple-element.109), channel_id=1, source_target_pairs={{1,0},{2,1},{3,2},{0,3},{5,4},{6,5},{7,6},{4,7},{9,8},{10,9},{11,1... | collective-permute-start | bytes 712712 | tf_op jit(solution)/shard_map/ppermute | solution.py:25
  67.8 7.2 %collective-permute-done.4 = f32[2,58,2,256]{3,1,2,0:T(8,128)S(1)} collective-permute-done((f32[2,58,2,256]{3,1,2,0:T(8,128)S(1)}, f32[2,58,2,256]{3,1,2,0:T(8,128)S(1)}, u32[]{:S(2)}, u32[]{:S(2)}) %collective-permute-start.4) | collective-permute-done | bytes 237600 | tf_op jit(solution)/shard_map/ppermute | solution.py:24
  75.0 2.3 %collective-permute-done.5 = f32[2,58,2,256]{3,1,2,0:T(8,128)S(1)} collective-permute-done((f32[2,58,2,256]{3,1,2,0:T(8,128)S(1)}, f32[2,58,2,256]{3,1,2,0:T(8,128)S(1)}, u32[]{:S(2)}, u32[]{:S(2)}) %collective-permute-start.5) | collective-permute-done | bytes 237600 | tf_op jit(solution)/shard_map/ppermute | solution.py:25
  78.2 2.2 %fusion.23 = f32[2,58,18,256]{3,1,2,0:T(8,128)S(1)} fusion(f32[1,58,16,256]{3,1,2,0:T(8,128)S(1)} %get-tuple-element.102, f32[1,58,16,256]{3,1,2,0:T(8,128)S(1)} %get-tuple-element.101, f32[2,58,2,256]{3,1,2,0:T(8,128)S(1)} %collective-permute-done.4, f32[2,58,2,256]{3,1,2,0:T(8,128)S(1)} %collective-permute-done.5, ...), kind=kLoop, calls=%fused_computation.109 | loop fusion | flops 18708480 | bytes 11032576 | tf_op jit(solution)/shard_map/add | solution.py:45
  81.1 1.7 %fusion.70 = f32[2,58,16,256]{3,1,2,0:T(8,128)S(1)} fusion(f32[1,58,18,256]{3,1,2,0:T(8,128)S(1)} %get-tuple-element.84, f32[1,58,18,256]{3,1,2,0:T(8,128)S(1)} %get-tuple-element.83, f32[2,1,16,256]{3,1,2,0:T(1,128)S(1)} %get-tuple-element.92, f32[2,57,16,256]{3,1,2,0:T(8,128)S(1)} %fusion.52, f32[2,1,16,256]{3,1,2,0:T(1,128)S(1)} %get-tuple-element.91, ...), kind=kLoop, calls=%fused_computation.167 | loop fusion | flops 9027584 | bytes 6150144 | tf_op jit(solution)/shard_map/add | solution.py:45
  83.2 1.7 %collective-permute-start.6 = (f32[2,58,2,256]{3,1,2,0:T(8,128)S(1)}, f32[2,58,2,256]{3,1,2,0:T(8,128)S(1)}, u32[]{:S(2)}, u32[]{:S(2)}) collective-permute-start(f32[2,58,2,256]{3,1,2,0:T(8,128)S(1)} %get-tuple-element.108), channel_id=1, source_target_pairs={{0,1},{1,2},{2,3},{3,0},{4,5},{5,6},{6,7},{7,4},{8,9},{9,10},{10,1... | collective-permute-start | bytes 712712 | tf_op jit(solution)/shard_map/ppermute | solution.py:24
  84.9 2.2 %collective-permute-start.7 = (f32[2,58,2,256]{3,1,2,0:T(8,128)S(1)}, f32[2,58,2,256]{3,1,2,0:T(8,128)S(1)}, u32[]{:S(2)}, u32[]{:S(2)}) collective-permute-start(f32[2,58,2,256]{3,1,2,0:T(8,128)S(1)} %get-tuple-element.107), channel_id=1, source_target_pairs={{1,0},{2,1},{3,2},{0,3},{5,4},{6,5},{7,6},{4,7},{9,8},{10,9},{11,1... | collective-permute-start | bytes 712712 | tf_op jit(solution)/shard_map/ppermute | solution.py:25
  87.1 1.9 %reduce_sum.38 = f32[2,58,256]{2,1,0:T(8,128)S(1)} reduce(f32[2,58,16,256]{3,2,1,0:T(8,128)} %param.11, f32[]{:T(128)} %constant.35.clone.1), dimensions={2}, to_apply=%region_8.9 | reduce | flops 445440 | bytes 2019332 | tf_op jit(solution)/shard_map/reduce_sum | solution.py:105
  89.0 5.3 %collective-permute-done.6 = f32[2,58,2,256]{3,1,2,0:T(8,128)S(1)} collective-permute-done((f32[2,58,2,256]{3,1,2,0:T(8,128)S(1)}, f32[2,58,2,256]{3,1,2,0:T(8,128)S(1)}, u32[]{:S(2)}, u32[]{:S(2)}) %collective-permute-start.6) | collective-permute-done | bytes 237600 | tf_op jit(solution)/shard_map/ppermute | solution.py:24
  94.3 3.6 %collective-permute-done.7 = f32[2,58,2,256]{3,1,2,0:T(8,128)S(1)} collective-permute-done((f32[2,58,2,256]{3,1,2,0:T(8,128)S(1)}, f32[2,58,2,256]{3,1,2,0:T(8,128)S(1)}, u32[]{:S(2)}, u32[]{:S(2)}) %collective-permute-start.7) | collective-permute-done | bytes 237600 | tf_op jit(solution)/shard_map/ppermute | solution.py:25
  98.7 2.0 %fusion.36 = f32[2,58,18,256]{3,1,2,0:T(8,128)S(1)} fusion(f32[1,58,16,256]{3,1,2,0:T(8,128)S(1)} %get-tuple-element.100, f32[1,58,16,256]{3,1,2,0:T(8,128)S(1)} %get-tuple-element.99, f32[2,58,2,256]{3,1,2,0:T(8,128)S(1)} %collective-permute-done.6, f32[2,58,2,256]{3,1,2,0:T(8,128)S(1)} %collective-permute-done.7, ...), kind=kLoop, calls=%fused_computation.122 | loop fusion | flops 18708480 | bytes 11032576 | tf_op jit(solution)/shard_map/add | solution.py:45
  101.5 1.7 %fusion.65 = f32[2,58,16,256]{3,1,2,0:T(8,128)S(1)} fusion(f32[1,58,18,256]{3,1,2,0:T(8,128)S(1)} %get-tuple-element.82, f32[1,58,18,256]{3,1,2,0:T(8,128)S(1)} %get-tuple-element.81, f32[2,1,16,256]{3,1,2,0:T(1,128)S(1)} %get-tuple-element.90, f32[2,57,16,256]{3,1,2,0:T(8,128)S(1)} %fusion.48, f32[2,1,16,256]{3,1,2,0:T(1,128)S(1)} %get-tuple-element.89, ...), kind=kLoop, calls=%fused_computation.161 | loop fusion | flops 9027584 | bytes 6150144 | tf_op jit(solution)/shard_map/add | solution.py:45
  103.8 0.7 sub.250
  104.5 33.6 %all-reduce.4.cloned.1.call-done = f32[2,58,256]{2,1,0:T(8,128)} async-done(((f32[2,58,256]{2,1,0:T(8,128)}), f32[2,58,256]{2,1,0:T(8,128)}) %all-reduce.4.cloned.1.call-update) | async-done | bytes 118800 | tf_op jit(solution)/shard_map/psum | solution.py:106
  138.1 0.9 multiply_bitcast_fusion
  139.2 1.2 scatter_custom_fusion.1
  140.3 0.7 reshape.78
  141.0 3.6 %all-to-all-start.2 = ((f32[8,34,116]{2,1,0:T(8,128)}), f32[8,34,116]{2,1,0:T(8,128)S(1)}, u32[]{:S(2)}, u32[]{:S(2)}) async-start(f32[8,34,116]{2,1,0:T(8,128)} %reshape.78), calls=%async_computation.2 | async-start | bytes 327680 | tf_op jit(solution)/shard_map/all_to_all | solution.py:112
  144.7 2.4 %copy.78 = f32[2,58,16,256]{3,2,1,0:T(8,128)} copy(f32[2,58,16,256]{3,1,2,0:T(8,128)S(1)} %get-tuple-element.105) | data formatting | bytes 3801088
  147.0 3.5 %all-to-all-done.2 = f32[8,34,116]{2,1,0:T(8,128)S(1)} async-done(((f32[8,34,116]{2,1,0:T(8,128)}), f32[8,34,116]{2,1,0:T(8,128)S(1)}, u32[]{:S(2)}, u32[]{:S(2)}) %all-to-all-start.2) | async-done | bytes 126240 | tf_op jit(solution)/shard_map/all_to_all | solution.py:112
  150.5 0.7 gather_fusion.4
  151.3 0.8 copy.77
  (92 shorter events, 11.5 us)
Async XLA Ops:
  7.2 15.6 %copy-start.2 = (s32[2048]{0:T(1024)S(1)}, s32[2048]{0:T(1024)}, u32[]{:S(2)}) copy-start(s32[2048]{0:T(1024)} %param.9) | copy-start | bytes 24580
  7.2 11.4 %copy-start = (f32[2,58,16,256]{3,2,1,0:T(8,128)S(1)}, f32[2,58,16,256]{3,2,1,0:T(8,128)}, u32[]{:S(2)}) copy-start(f32[2,58,16,256]{3,2,1,0:T(8,128)} %param.11) | copy-start | bytes 5701636
  11.4 13.0 %copy-start.3 = (s32[256]{0:T(256)S(1)}, s32[256]{0:T(256)}, u32[]{:S(2)}) copy-start(s32[256]{0:T(256)} %param.10) | copy-start | bytes 3076
  11.4 13.0 %copy-start.1 = (f32[256,116]{0,1:T(8,128)S(1)}, f32[256,116]{0,1:T(8,128)}, u32[]{:S(2)}) copy-start(f32[256,116]{0,1:T(8,128)} %param.7) | copy-start | bytes 356356
  13.4 12.9 %all-to-all-start = ((f32[8,1,1972]{2,1,0:T(1,128)}), f32[8,1,1972]{2,1,0:T(1,128)S(1)}, u32[]{:S(2)}, u32[]{:S(2)}) async-start(f32[8,1,1972]{2,1,0:T(1,128)} %reshape.148), calls=%async_computation | async-start | bytes 131072 | tf_op jit(solution)/shard_map/all_to_all | solution.py:74
  18.8 18.4 %collective-permute-start = (f32[2,58,2,256]{3,1,2,0:T(8,128)S(1)}, f32[2,58,2,256]{3,1,2,0:T(8,128)S(1)}, u32[]{:S(2)}, u32[]{:S(2)}) collective-permute-start(f32[2,58,2,256]{3,1,2,0:T(8,128)S(1)} %copy.84), channel_id=1, source_target_pairs={{0,1},{1,2},{2,3},{3,0},{4,5},{5,6},{6,7},{7,4},{8,9},{9,10},{10,1... | collective-permute-start | bytes 712712 | tf_op jit(solution)/shard_map/ppermute | solution.py:24
  20.5 18.2 %collective-permute-start.1 = (f32[2,58,2,256]{3,1,2,0:T(8,128)S(1)}, f32[2,58,2,256]{3,1,2,0:T(8,128)S(1)}, u32[]{:S(2)}, u32[]{:S(2)}) collective-permute-start(f32[2,58,2,256]{3,1,2,0:T(8,128)S(1)} %copy.85), channel_id=1, source_target_pairs={{1,0},{2,1},{3,2},{0,3},{5,4},{6,5},{7,6},{4,7},{9,8},{10,9},{11,1... | collective-permute-start | bytes 712712 | tf_op jit(solution)/shard_map/ppermute | solution.py:25
  26.3 10.0 %all-to-all-start.1 = ((f32[8,34,116]{2,1,0:T(8,128)}), f32[8,34,116]{2,1,0:T(8,128)S(1)}, u32[]{:S(2)}, u32[]{:S(2)}) async-start(f32[8,34,116]{2,1,0:T(8,128)} %reshape.75), calls=%async_computation.1 | async-start | bytes 327680 | tf_op jit(solution)/shard_map/all_to_all | solution.py:73
  30.5 107.6 %all-reduce.4.cloned.1.call-start = ((), (), s32[]{:S(2)}) async-start(), calls=%async_computation.3 | async-start | bytes 262144 | tf_op jit(solution)/shard_map/psum | solution.py:106
  44.2 11.0 %collective-permute-start.2 = (f32[2,58,2,256]{3,1,2,0:T(8,128)S(1)}, f32[2,58,2,256]{3,1,2,0:T(8,128)S(1)}, u32[]{:S(2)}, u32[]{:S(2)}) collective-permute-start(f32[2,58,2,256]{3,1,2,0:T(8,128)S(1)} %get-tuple-element.112), channel_id=1, source_target_pairs={{0,1},{1,2},{2,3},{3,0},{4,5},{5,6},{6,7},{7,4},{8,9},{9,10},{10,1... | collective-permute-start | bytes 712712 | tf_op jit(solution)/shard_map/ppermute | solution.py:24
  44.3 13.6 %collective-permute-start.3 = (f32[2,58,2,256]{3,1,2,0:T(8,128)S(1)}, f32[2,58,2,256]{3,1,2,0:T(8,128)S(1)}, u32[]{:S(2)}, u32[]{:S(2)}) collective-permute-start(f32[2,58,2,256]{3,1,2,0:T(8,128)S(1)} %get-tuple-element.111), channel_id=1, source_target_pairs={{1,0},{2,1},{3,2},{0,3},{5,4},{6,5},{7,6},{4,7},{9,8},{10,9},{11,1... | collective-permute-start | bytes 712712 | tf_op jit(solution)/shard_map/ppermute | solution.py:25
  63.9 11.0 %collective-permute-start.4 = (f32[2,58,2,256]{3,1,2,0:T(8,128)S(1)}, f32[2,58,2,256]{3,1,2,0:T(8,128)S(1)}, u32[]{:S(2)}, u32[]{:S(2)}) collective-permute-start(f32[2,58,2,256]{3,1,2,0:T(8,128)S(1)} %get-tuple-element.110), channel_id=1, source_target_pairs={{0,1},{1,2},{2,3},{3,0},{4,5},{5,6},{6,7},{7,4},{8,9},{9,10},{10,1... | collective-permute-start | bytes 712712 | tf_op jit(solution)/shard_map/ppermute | solution.py:24
  64.8 12.4 %collective-permute-start.5 = (f32[2,58,2,256]{3,1,2,0:T(8,128)S(1)}, f32[2,58,2,256]{3,1,2,0:T(8,128)S(1)}, u32[]{:S(2)}, u32[]{:S(2)}) collective-permute-start(f32[2,58,2,256]{3,1,2,0:T(8,128)S(1)} %get-tuple-element.109), channel_id=1, source_target_pairs={{1,0},{2,1},{3,2},{0,3},{5,4},{6,5},{7,6},{4,7},{9,8},{10,9},{11,1... | collective-permute-start | bytes 712712 | tf_op jit(solution)/shard_map/ppermute | solution.py:25
  83.2 11.1 %collective-permute-start.6 = (f32[2,58,2,256]{3,1,2,0:T(8,128)S(1)}, f32[2,58,2,256]{3,1,2,0:T(8,128)S(1)}, u32[]{:S(2)}, u32[]{:S(2)}) collective-permute-start(f32[2,58,2,256]{3,1,2,0:T(8,128)S(1)} %get-tuple-element.108), channel_id=1, source_target_pairs={{0,1},{1,2},{2,3},{3,0},{4,5},{5,6},{6,7},{7,4},{8,9},{9,10},{10,1... | collective-permute-start | bytes 712712 | tf_op jit(solution)/shard_map/ppermute | solution.py:24
  84.9 13.0 %collective-permute-start.7 = (f32[2,58,2,256]{3,1,2,0:T(8,128)S(1)}, f32[2,58,2,256]{3,1,2,0:T(8,128)S(1)}, u32[]{:S(2)}, u32[]{:S(2)}) collective-permute-start(f32[2,58,2,256]{3,1,2,0:T(8,128)S(1)} %get-tuple-element.107), channel_id=1, source_target_pairs={{1,0},{2,1},{3,2},{0,3},{5,4},{6,5},{7,6},{4,7},{9,8},{10,9},{11,1... | collective-permute-start | bytes 712712 | tf_op jit(solution)/shard_map/ppermute | solution.py:25
  141.0 9.5 %all-to-all-start.2 = ((f32[8,34,116]{2,1,0:T(8,128)}), f32[8,34,116]{2,1,0:T(8,128)S(1)}, u32[]{:S(2)}, u32[]{:S(2)}) async-start(f32[8,34,116]{2,1,0:T(8,128)} %reshape.78), calls=%async_computation.2 | async-start | bytes 327680 | tf_op jit(solution)/shard_map/all_to_all | solution.py:112
Sparse Core Ops, SparseCore 0:
  104.6 33.4 all-reduce.3
where the time goes:
time: 159 us
  waiting for transfers between devices  68.8 us (43%)
  starting transfers between devices  28.6 us (18%)
  other arithmetic  28 us (18%)
  local copies, waits for them, and re-layouts  18.8 us (12%)
  between operations  14.7 us (9%)
    psum x1, waiting for transfers between devices, on_device(): totals = lax.psum(partial_value, 'grp')  33.6 us
    ppermute x4, waiting for transfers between devices, padded(): before = lax.ppermute(last, axis, up)  19.6 us
    add x8, other arithmetic, advance(): centre + courant_here * ((western - eastern) * 0.5)  14.8 us
    ppermute x4, starting transfers between devices, padded(): after = lax.ppermute(leading, axis, down)  11.3 us
    ppermute x4, waiting for transfers between devices, padded(): after = lax.ppermute(leading, axis, down)  8.53 us
    unnamed x20, local copies, waits for them, and re-layouts  6.61 us
    all_to_all x1, starting transfers between devices, on_device(): lax.all_to_all(out_cour, 'col', split_axis=0, concat_axis=0, tiled=True)  5.2 us
    ppermute x4, starting transfers between devices, padded(): before = lax.ppermute(last, axis, up)  4.23 us
  transfers between devices with their start and end apart: 12, of which 9 were waited for; matrix products, arithmetic and copies ran while one was open for 8% of the time, Pallas kernels for 0%

commit v1 on v0

v1 whole, which is shorter than its diff:
```python
import functools

import jax
import jax.numpy as jnp
from jax import lax
from jax.experimental import pallas as pl
from jax.experimental.pallas import tpu as pltpu
from jax.sharding import PartitionSpec as P

STEPS = 8
LANES = 128
MESH = pl.DeviceIdType.MESH
HIGHEST = lax.Precision.HIGHEST

diffuse_x = 0.25
diffuse_z = 0.2
sat_scale = 0.5
sat_slope = 0.3
cond_rate = 0.5
latent_gain = 0.4
LOG2E = 1.4426950408889634


def round_up(n, m):
    return -(-n // m) * m


def cloud_kernel(halo, x_ref, left_ref, right_ref, force_ref, cour_ref, cloud_ref, *rest):
    out_ref, part_ref, buf = rest[-3:]
    levels, cells = x_ref.shape[1:3]
    width = cells + 2 * halo
    half_cloud = cond_rate * cloud_ref[...]

    zeros = jnp.zeros((8, LANES), jnp.float32)

    def fill(z, carry):
        for f in range(2):
            buf[0, f, z, 8 : 8 + halo] = left_ref[f, z]
            buf[0, f, z, 8 + halo : 8 + halo + cells] = x_ref[f, z]
            buf[0, f, z, 8 + halo + cells : 8 + width] = right_ref[f, z]
            for b in range(2):
                buf[b, f, z, 0:8] = zeros
                buf[b, f, z, 8 + width : 16 + width] = zeros
        return carry

    lax.fori_loop(0, levels, fill, 0)

    def stepped(src, z, first, count):
        up = jnp.minimum(z + 1, levels - 1)
        down = jnp.maximum(z - 1, 0)
        c = cour_ref[pl.ds(z, 1), :]
        to_east = diffuse_x + 0.5 * c
        to_west = diffuse_x - 0.5 * c
        new = []
        for f in range(2):
            here = buf[src, f, z, first : first + count]
            west = buf[src, f, z, first - 1 : first + count - 1]
            east = buf[src, f, z, first + 1 : first + count + 1]
            upper = buf[src, f, up, first : first + count]
            lower = buf[src, f, down, first : first + count]
            new.append(
                (1.0 - 2.0 * diffuse_x - 2.0 * diffuse_z) * here
                + (to_east * west + to_west * east)
                + (diffuse_z * (upper + lower) + force_ref[f, pl.ds(z, 1), :])
            )
        energy, moisture = new
        excess = (moisture + sat_scale) - sat_scale * jnp.exp2((sat_slope * LOG2E) * energy)
        amount = jnp.maximum(excess, 0.0) * half_cloud
        return energy + latent_gain * amount, moisture - amount

    def sweep(src, dst):
        def level(z, carry):
            energy, moisture = stepped(src, z, 8, width)
            buf[dst, 0, z, 8 : 8 + width] = energy
            buf[dst, 1, z, 8 : 8 + width] = moisture
            return carry

        lax.fori_loop(0, levels, level, 0, unroll=2)

    sweep(0, 1)

    def pair(i, carry):
        sweep(1, 0)
        sweep(0, 1)
        return carry

    lax.fori_loop(0, (STEPS - 2) // 2, pair, 0)

    def last(z, carry):
        for f, value in enumerate(stepped(1, z, 8 + halo, cells)):
            out_ref[f, z] = value
            part_ref[f, pl.ds(z, 1), :] = jnp.sum(value - x_ref[f, z], axis=0, keepdims=True)
        return carry

    lax.fori_loop(0, levels, last, 0, unroll=2)


def run_cloud(chunk, state, left, right, forcing, courant_here, cloudy, so_far):
    fields, levels, cells, columns = state.shape
    halo = left.shape[2]
    wide = lambda n: pl.BlockSpec((fields, levels, n, LANES), lambda i: (0, 0, 0, chunk))
    one = lambda n: pl.BlockSpec((fields, levels, n, LANES), lambda i: (0, 0, 0, 0))
    in_specs = [
        wide(cells),
        one(halo),
        one(halo),
        pl.BlockSpec((fields, levels, LANES), lambda i: (0, 0, chunk)),
        pl.BlockSpec((levels, LANES), lambda i: (0, chunk)),
        pl.BlockSpec((1, LANES), lambda i: (0, chunk)),
    ]
    args = [state, left, right, forcing, courant_here, cloudy]
    aliases = {}
    if so_far is not None:
        in_specs.append(pl.BlockSpec(memory_space=pl.ANY))
        args.append(so_far)
        aliases = {6: 0}
    work = fields * levels * (cells + 2 * halo) * LANES
    return pl.pallas_call(
        functools.partial(cloud_kernel, halo),
        grid=(1,),
        out_shape=(
            jax.ShapeDtypeStruct(state.shape, jnp.float32),
            jax.ShapeDtypeStruct((fields, levels, LANES), jnp.float32),
        ),
        in_specs=in_specs,
        out_specs=(wide(cells), pl.BlockSpec((fields, levels, LANES), lambda i: (0, 0, 0))),
        scratch_shapes=[pltpu.VMEM((2, fields, levels, cells + 2 * halo + 16, LANES), jnp.float32)],
        input_output_aliases=aliases,
        compiler_params=pltpu.CompilerParams(vmem_limit_bytes=40 * 2**20),
        cost_estimate=pl.CostEstimate(
            flops=28 * STEPS * work // 2, bytes_accessed=8 * work, transcendentals=STEPS * work // 2
        ),
    )(*args)


def tail_kernel(cells_all, part_ref, t_ref, r_ref, out_ref, mine, inc, heap, pack, land, sems):
    rows, lanes = part_ref.shape
    groups, cap = land.shape[:2]
    grp_count = lax.axis_size("grp")
    share = rows // grp_count
    z = lax.axis_index("grp")
    c = lax.axis_index("col")
    barrier = pltpu.get_barrier_semaphore()
    for k in range(1, grp_count):
        pl.semaphore_signal(
            barrier, inc=1, device_id={"grp": lax.rem(z + k, grp_count)}, device_id_type=MESH
        )
    for k in range(1, groups):
        pl.semaphore_signal(
            barrier, inc=1, device_id={"col": lax.rem(c + k, groups)}, device_id_type=MESH
        )
    pl.semaphore_wait(barrier, grp_count - 1 + groups - 1)

    def block(i):
        return pl.ds(pl.multiple_of(i * share, share), share)

    scatter = []
    for k in range(1, grp_count):
        peer = lax.rem(z + k, grp_count)
        copy = pltpu.make_async_remote_copy(
            src_ref=part_ref.at[block(peer)],
            dst_ref=heap.at[k - 1],
            send_sem=sems.at[0, k],
            recv_sem=sems.at[1, k],
            device_id={"grp": peer},
            device_id_type=MESH,
        )
        copy.start()
        scatter.append(copy)
    total = part_ref[block(z), :]
    for k, copy in enumerate(scatter):
        copy.wait_recv()
        total = total + heap[k]
    mine[...] = total / cells_all
    inc[block(z), :] = total / cells_all
    spread = []
    for k in range(1, grp_count):
        copy = pltpu.make_async_remote_copy(
            src_ref=mine,
            dst_ref=inc.at[block(z)],
            send_sem=sems.at[2, k],
            recv_sem=sems.at[3, k],
            device_id={"grp": lax.rem(z + k, grp_count)},
            device_id_type=MESH,
        )
        copy.start()
        spread.append(copy)
    for copy in spread:
        copy.wait_recv()
    pack[...] = jnp.dot(
        t_ref[...], inc[...], precision=HIGHEST, preferred_element_type=jnp.float32
    ).reshape(groups, cap, lanes)
    returns = []
    for k in range(1, groups):
        peer = lax.rem(c + k, groups)
        copy = pltpu.make_async_remote_copy(
            src_ref=pack.at[peer],
            dst_ref=land.at[c],
            send_sem=sems.at[4, k],
            recv_sem=sems.at[5, k],
            device_id={"col": peer},
            device_id_type=MESH,
        )
        copy.start()
        returns.append(copy)
    land[c] = pack[c]
    for copy in returns:
        copy.wait_recv()
    out = lax.dot_general(
        r_ref[...],
        land[...].reshape(groups * cap, lanes),
        (((0,), (0,)), ((), ())),
        precision=HIGHEST,
        preferred_element_type=jnp.float32,
    )
    out_ref[...] = out[:, : out_ref.shape[1]]
    for copy in scatter + spread + returns:
        copy.wait_send()


def run_tail(cells_all, partial, take, give, width):
    rows, lanes = partial.shape
    groups = lax.axis_size("col")
    grp_count = lax.axis_size("grp")
    cap = take.shape[0] // groups
    vmem = pl.BlockSpec(memory_space=pltpu.VMEM)
    return pl.pallas_call(
        functools.partial(tail_kernel, cells_all),
        out_shape=jax.ShapeDtypeStruct((rows, width), jnp.float32),
        in_specs=[vmem] * 3,
        out_specs=vmem,
        scratch_shapes=[
            pltpu.VMEM((rows // grp_count, lanes), jnp.float32),
            pltpu.VMEM((rows, lanes), jnp.float32),
            pltpu.VMEM((grp_count - 1, rows // grp_count, lanes), jnp.float32),
            pltpu.VMEM((groups, cap, lanes), jnp.float32),
            pltpu.VMEM((groups, cap, lanes), jnp.float32),
            pltpu.SemaphoreType.DMA((6, max(grp_count, groups))),
        ],
        compiler_params=pltpu.CompilerParams(collective_id=0, has_side_effects=True),
    )(partial, take, give)


def ring_halo(part, depth):
    peers, cells = lax.axis_size("grp"), part.shape[2]
    lefts, rights = [], []
    need, hop = depth, 1
    while need > 0:
        n = min(need, cells)
        up = [(i, (i + hop) % peers) for i in range(peers)]
        down = [(j, i) for i, j in up]
        lefts.insert(0, lax.ppermute(part[:, :, cells - n :], "grp", up))
        rights.append(lax.ppermute(part[:, :, :n], "grp", down))
        need, hop = need - n, hop + 1
    join = lambda xs: xs[0] if len(xs) == 1 else jnp.concatenate(xs, axis=2)
    return join(lefts), join(rights)


def on_device(profiles, courant, owner_map, cloud_flags, crm_state):
    columns = profiles.shape[0]
    levels = courant.shape[1]
    groups = lax.axis_size("col")
    me = lax.axis_index("col")
    per_peer = columns // groups
    cap = round_up(per_peer + min(2, per_peer), 8)
    chunks = columns // LANES

    halos = []
    for i in range(chunks):
        halos.append(ring_halo(crm_state[..., i * LANES : (i + 1) * LANES], STEPS))

    ids = jnp.arange(groups, dtype=jnp.int32)
    slots = jnp.arange(cap, dtype=jnp.int32)
    spots = jnp.arange(columns, dtype=jnp.int32)
    earlier = (spots[:, None] < spots[None, :]).astype(jnp.float32)
    mine = lax.dynamic_slice_in_dim(owner_map, me * columns, columns)
    blocks = owner_map.reshape(groups, columns)

    def places(hits):
        rank = jnp.dot(hits.astype(jnp.float32), earlier).astype(jnp.int32)
        return hits[:, None, :] & (rank[:, None, :] == slots[None, :, None])

    give = places((mine // columns)[None, :] == ids[:, None])
    give = give.reshape(groups * cap, columns).astype(jnp.float32)
    landing = places(blocks // columns == me)
    spot = jnp.sum(jnp.where(landing, (blocks - me * columns + 1)[:, None, :], 0), axis=2)
    take = (spot.reshape(groups * cap)[:, None] == spots[None, :] + 1).astype(jnp.float32)

    both = jnp.concatenate([profiles, courant], axis=1)
    out = jnp.dot(give, both, precision=HIGHEST).reshape(groups, cap, 3 * levels)
    got = lax.all_to_all(out, "col", split_axis=0, concat_axis=0, tiled=True)
    phys = lax.dot_general(
        got.reshape(groups * cap, 3 * levels), take, (((0,), (0,)), ((), ())), precision=HIGHEST
    )
    forcing = phys[: 2 * levels].reshape(2, levels, columns) / STEPS
    courant_here = phys[2 * levels :]
    cloudy = cloud_flags.astype(jnp.float32)[None, :]

    final, parts = None, []
    for i, (left, right) in enumerate(halos):
        final, part = run_cloud(
            i, crm_state, left, right, forcing, courant_here, cloudy, final
        )
        parts.append(part.reshape(2 * levels, LANES).T)
    partial = jnp.concatenate(parts, axis=0)
    partial = jnp.pad(partial, ((0, 0), (0, round_up(2 * levels, LANES) - 2 * levels)))
    cells_all = crm_state.shape[2] * lax.axis_size("grp")
    tendency = run_tail(float(cells_all), partial, take, give, 2 * levels)
    return tendency, final


def solution(mesh):
    placed = (P("col", None), P("col", None), P(), P("col"), P(None, None, "grp", "col"))
    return jax.shard_map(
        on_device,
        mesh=mesh,
        in_specs=placed,
        out_specs=(P("col", None), P(None, None, "grp", "col")),
        check_vma=False,
    )
```

time: 159 us -> 91.5 us (0.58)
  waiting for transfers between devices: 68.8 us -> 20.5 us
  Pallas kernels: 0 us -> 46 us
  other arithmetic: 28 us -> 3.42 us
  starting transfers between devices: 28.6 us -> 12.8 us
  local copies, waits for them, and re-layouts: 18.8 us -> 4.82 us
  between operations: 14.7 us -> 0.74 us
  matrix products: 0 us -> 2.84 us
    pallas_call x0 -> x3, Pallas kernels: none -> 46 us  [the longest x2 27.4 us: run_cloud(): pl.pallas_call(functools.partial(cloud_kernel, halo), grid=(1,), out_shap...]
    psum x1 -> x0, waiting for transfers between devices: 33.6 us -> none  [on_device(): totals = lax.psum(partial_value, 'grp')]
    add x16 -> x2, other arithmetic: 17.2 us -> 0.01 us  [the longest x1 0.01 us: on_device(): blocks - me * columns + 1]
    ppermute x8 -> x4, starting transfers between devices: 15.6 us -> 7.65 us  [the longest x2 6.07 us: ring_halo(): rights.append(lax.ppermute(part[:, :, :n], 'grp', down))]
    all_to_all x3 -> x1, starting transfers between devices: 13 us -> 5.2 us  [on_device(): got = lax.all_to_all(out, 'col', split_axis=0, concat_axis=0, tiled=True)]
    ppermute x8 -> x4, waiting for transfers between devices: 28.1 us -> 20.5 us  [the longest x2 15.1 us: ring_halo(): rights.append(lax.ppermute(part[:, :, :n], 'grp', down))]
    all_to_all x3 -> x1, waiting for transfers between devices: 7 us -> 0.01 us  [on_device(): got = lax.all_to_all(out, 'col', split_axis=0, concat_axis=0, tiled=True)]
    unnamed x20 -> x7, local copies, waits for them, and re-layouts: 6.61 us -> 1.68 us
  transfers between devices with their start and end apart: 12 -> 5, of which waited for: 9 -> 3; matrix products, arithmetic and copies ran while one was open for 8% -> 6% of each run, Pallas kernels for 0% -> 16%
where the time goes in v1:
time: 91.5 us; the launch traced here: 91.1 us
  Pallas kernels  46 us (50%)
  waiting for transfers between devices  20.5 us (22%)
  starting transfers between devices  12.8 us (14%)
  local copies, waits for them, and re-layouts  4.82 us (5%)
  other arithmetic  3.42 us (4%)
  matrix products  2.84 us (3%)
    pallas_call x2, Pallas kernels, run_cloud(): pl.pallas_call(functools.partial(cloud_kernel, halo), grid=(1,), out_shap...  27.4 us
    pallas_call x1, Pallas kernels, run_tail(): pl.pallas_call(functools.partial(tail_kernel, cells_all), out_shape=jax.S...  18.6 us
    ppermute x2, waiting for transfers between devices, ring_halo(): rights.append(lax.ppermute(part[:, :, :n], 'grp', down))  15.1 us
    ppermute x2, starting transfers between devices, ring_halo(): rights.append(lax.ppermute(part[:, :, :n], 'grp', down))  6.07 us
    ppermute x2, waiting for transfers between devices, ring_halo(): lefts.insert(0, lax.ppermute(part[:, :, cells - n:], 'grp', up))  5.34 us
    all_to_all x1, starting transfers between devices, on_device(): got = lax.all_to_all(out, 'col', split_axis=0, concat_axis=0, tiled=True)  5.2 us
    slice x1, local copies, waits for them, and re-layouts, ring_halo(): rights.append(lax.ppermute(part[:, :, :n], 'grp', down))  2.76 us
    dot_general x1, matrix products, on_device(): jnp.dot(give, both, precision=HIGHEST).reshape(groups, cap, 3 * levels)  2 us
  transfers between devices with their start and end apart: 5, of which 3 were waited for; matrix products, arithmetic and copies ran while one was open for 6% of the time, Pallas kernels for 16%

profile of v1, /device:TPU:0, one launch (start us, length us, event | category | flops | bytes accessed | tf_op | source)
XLA Modules:
  0.0 91.1 jit_solution(1359090457817237484)
XLA Ops:
  0.6 0.8 and_select_fusion
  1.4 0.1 convolution_convert_fusion.1
  1.6 2.0 %fusion.3 = f32[8,40,174]{2,1,0:T(8,128)} fusion(f32[256,58]{0,1:T(8,128)} %param.6, f32[256,116]{0,1:T(8,128)} %param.5, s32[8,256]{1,0:T(8,128)S(1)} %convolution_convert_fusion.1, pred[8,256]{1,0:T(8,128)(4,1)S(1)} %iota_compare_fusion.6), kind=kOutput, calls=%fused_computation.10 | convolution fusion | flops 171257344 | bytes 411136 | tf_op jit(solution)/shard_map/dot_general | solution.py:290
  3.6 5.2 %all-to-all-start = ((f32[8,40,174]{2,1,0:T(8,128)}), f32[8,40,174]{2,1,0:T(8,128)S(1)}, u32[]{:S(2)}, u32[]{:S(2)}) async-start(f32[8,40,174]{2,1,0:T(8,128)} %fusion.3), calls=%async_computation | async-start | bytes 655360 | tf_op jit(solution)/shard_map/all_to_all | solution.py:291
  8.8 0.0 copy-start.1
  8.8 0.0 copy-start.2
  8.8 2.8 %fusion.18 = (f32[2,58,8,128]{3,2,1,0:T(8,128)}, f32[2,58,8,128]{3,2,1,0:T(8,128)}, f32[2,58,8,128]{3,2,1,0:T(8,128)}, f32[2,58,8,128]{3,2,1,0:T(8,128)}) fusion(f32[2,58,16,256]{3,2,1,0:T(8,128)} %x_ref.3), kind=kLoop, calls=%fused_computation.41 | loop fusion | bytes 3801088 | tf_op jit(solution)/shard_map/slice | solution.py:253
  11.5 0.0 copy-start
  11.5 1.6 %collective-permute-start = (f32[2,58,8,128]{3,2,1,0:T(8,128)}, f32[2,58,8,128]{3,2,1,0:T(8,128)}, u32[]{:S(2)}, u32[]{:S(2)}) collective-permute-start(f32[2,58,8,128]{3,2,1,0:T(8,128)} %get-tuple-element.18), channel_id=1, source_target_pairs={{0,1},{1,2},{2,3},{3,0},{4,5},{5,6},{6,7},{7,4},{8,9},{9,10},{10,1... | collective-permute-start | bytes 1425416 | tf_op jit(solution)/shard_map/ppermute | solution.py:252
  13.1 2.2 %collective-permute-start.1 = (f32[2,58,8,128]{3,2,1,0:T(8,128)}, f32[2,58,8,128]{3,2,1,0:T(8,128)}, u32[]{:S(2)}, u32[]{:S(2)}) collective-permute-start(f32[2,58,8,128]{3,2,1,0:T(8,128)} %get-tuple-element.16), channel_id=1, source_target_pairs={{1,0},{2,1},{3,2},{0,3},{5,4},{6,5},{7,6},{4,7},{9,8},{10,9},{11,1... | collective-permute-start | bytes 1425416 | tf_op jit(solution)/shard_map/ppermute | solution.py:253
  15.4 0.0 collective-permute-start.2
  15.4 3.8 %collective-permute-start.3 = (f32[2,58,8,128]{3,2,1,0:T(8,128)}, f32[2,58,8,128]{3,2,1,0:T(8,128)S(1)}, u32[]{:S(2)}, u32[]{:S(2)}) collective-permute-start(f32[2,58,8,128]{3,2,1,0:T(8,128)} %get-tuple-element.19), channel_id=1, source_target_pairs={{1,0},{2,1},{3,2},{0,3},{5,4},{6,5},{7,6},{4,7},{9,8},{10,9},{11,1... | collective-permute-start | bytes 1425416 | tf_op jit(solution)/shard_map/ppermute | solution.py:253
  19.2 0.0 copy-done.1
  19.2 0.1 convolution_convert_fusion
  19.4 0.2 select_reduce_fusion
  19.6 0.1 eq.91
  19.7 0.8 compare_convert_fusion.t_ref
  20.5 0.0 copy-done.2
  20.6 0.1 eq.97
  20.6 0.9 fusion.7.r_ref
  21.5 0.0 all-to-all-done
  21.5 0.5 fusion
  22.1 5.3 %collective-permute-done.left_ref = f32[2,58,8,128]{3,2,1,0:T(8,128)} collective-permute-done((f32[2,58,8,128]{3,2,1,0:T(8,128)}, f32[2,58,8,128]{3,2,1,0:T(8,128)}, u32[]{:S(2)}, u32[]{:S(2)}) %collective-permute-start) | collective-permute-done | bytes 475168 | tf_op jit(solution)/shard_map/ppermute | solution.py:252
  27.4 10.2 %collective-permute-done.1.right_ref = f32[2,58,8,128]{3,2,1,0:T(8,128)} collective-permute-done((f32[2,58,8,128]{3,2,1,0:T(8,128)}, f32[2,58,8,128]{3,2,1,0:T(8,128)}, u32[]{:S(2)}, u32[]{:S(2)}) %collective-permute-start.1) | collective-permute-done | bytes 475168 | tf_op jit(solution)/shard_map/ppermute | solution.py:253
  37.7 0.0 copy-done
  37.7 14.3 %shard_map.68 = (f32[2,58,16,256]{3,2,1,0:T(8,128)}, f32[2,58,128]{2,1,0:T(8,128)S(1)}) custom-call(f32[2,58,16,256]{3,2,1,0:T(8,128)S(1)} %copy-done, f32[2,58,8,128]{3,2,1,0:T(8,128)} %collective-permute-done.left_ref, f32[2,58,8,128]{3,2,1,0:T(8,128)} %collective-permute-done.1.right_ref, f32[2,58,256]{2,1,0:T(8,128)S(1)} %div.42.force_ref, ...), custom_call_target="tpu_custom_call" | custom-call | flops 53215232 | bytes 3801088 | tf_op jit(solution)/shard_map/pallas_call | solution.py:118
  52.0 0.0 collective-permute-done.2.left_ref
  52.0 4.9 %collective-permute-done.3.right_ref = f32[2,58,8,128]{3,2,1,0:T(8,128)S(1)} collective-permute-done((f32[2,58,8,128]{3,2,1,0:T(8,128)}, f32[2,58,8,128]{3,2,1,0:T(8,128)S(1)}, u32[]{:S(2)}, u32[]{:S(2)}) %collective-permute-start.3) | collective-permute-done | bytes 475168 | tf_op jit(solution)/shard_map/ppermute | solution.py:253
  56.9 13.1 %shard_map.69 = (f32[2,58,16,256]{3,2,1,0:T(8,128)}, f32[2,58,128]{2,1,0:T(8,128)S(1)}) custom-call(f32[2,58,16,256]{3,2,1,0:T(8,128)S(1)} %copy-done, f32[2,58,8,128]{3,2,1,0:T(8,128)S(1)} %collective-permute-done.2.left_ref, f32[2,58,8,128]{3,2,1,0:T(8,128)S(1)} %collective-permute-done.3.right_ref, ...), custom_call_target="tpu_custom_call", output_to_operand_aliasing={{0}: (6, {})} | custom-call | flops 53215232 | bytes 3801088 | tf_op jit(solution)/shard_map/pallas_call | solution.py:118
  70.0 0.1 copy.15
  70.1 0.1 copy.14
  70.2 0.7 select_maximum_fusion.part_ref
  70.9 18.6 %shard_map.70 = f32[256,116]{1,0:T(8,128)} custom-call(f32[256,128]{1,0:T(8,128)} %select_maximum_fusion.part_ref, f32[320,256]{1,0:T(8,128)} %compare_convert_fusion.t_ref, f32[320,256]{1,0:T(8,128)} %fusion.7.r_ref), custom_call_target="tpu_custom_call" | custom-call | tf_op jit(solution)/shard_map/pallas_call | solution.py:227
  89.5 1.7 %copy.16 = f32[256,116]{0,1:T(8,128)} copy(f32[256,116]{1,0:T(8,128)} %shard_map.70) | data formatting | bytes 237568
  (12 shorter events, 0.1 us)
Async XLA Ops:
  3.6 17.9 %all-to-all-start = ((f32[8,40,174]{2,1,0:T(8,128)}), f32[8,40,174]{2,1,0:T(8,128)S(1)}, u32[]{:S(2)}, u32[]{:S(2)}) async-start(f32[8,40,174]{2,1,0:T(8,128)} %fusion.3), calls=%async_computation | async-start | bytes 655360 | tf_op jit(solution)/shard_map/all_to_all | solution.py:291
  8.8 10.4 %copy-start.1 = (s32[2048]{0:T(1024)S(1)}, s32[2048]{0:T(1024)}, u32[]{:S(2)}) copy-start(s32[2048]{0:T(1024)} %param.7) | copy-start | bytes 24580
  8.8 11.8 %copy-start.2 = (s32[256]{0:T(256)S(1)}, s32[256]{0:T(256)}, u32[]{:S(2)}) copy-start(s32[256]{0:T(256)} %param.8) | copy-start | bytes 3076
  11.5 26.2 %copy-start = (f32[2,58,16,256]{3,2,1,0:T(8,128)S(1)}, f32[2,58,16,256]{3,2,1,0:T(8,128)}, u32[]{:S(2)}) copy-start(f32[2,58,16,256]{3,2,1,0:T(8,128)} %x_ref.3) | copy-start | bytes 5701636
  11.5 15.9 %collective-permute-start = (f32[2,58,8,128]{3,2,1,0:T(8,128)}, f32[2,58,8,128]{3,2,1,0:T(8,128)}, u32[]{:S(2)}, u32[]{:S(2)}) collective-permute-start(f32[2,58,8,128]{3,2,1,0:T(8,128)} %get-tuple-element.18), channel_id=1, source_target_pairs={{0,1},{1,2},{2,3},{3,0},{4,5},{5,6},{6,7},{7,4},{8,9},{9,10},{10,1... | collective-permute-start | bytes 1425416 | tf_op jit(solution)/shard_map/ppermute | solution.py:252
  13.1 24.6 %collective-permute-start.1 = (f32[2,58,8,128]{3,2,1,0:T(8,128)}, f32[2,58,8,128]{3,2,1,0:T(8,128)}, u32[]{:S(2)}, u32[]{:S(2)}) collective-permute-start(f32[2,58,8,128]{3,2,1,0:T(8,128)} %get-tuple-element.16), channel_id=1, source_target_pairs={{1,0},{2,1},{3,2},{0,3},{5,4},{6,5},{7,6},{4,7},{9,8},{10,9},{11,1... | collective-permute-start | bytes 1425416 | tf_op jit(solution)/shard_map/ppermute | solution.py:253
  15.4 36.6 %collective-permute-start.2 = (f32[2,58,8,128]{3,2,1,0:T(8,128)}, f32[2,58,8,128]{3,2,1,0:T(8,128)S(1)}, u32[]{:S(2)}, u32[]{:S(2)}) collective-permute-start(f32[2,58,8,128]{3,2,1,0:T(8,128)} %get-tuple-element.17), channel_id=1, source_target_pairs={{0,1},{1,2},{2,3},{3,0},{4,5},{5,6},{6,7},{7,4},{8,9},{9,10},{10,1... | collective-permute-start | bytes 1425416 | tf_op jit(solution)/shard_map/ppermute | solution.py:252
  15.4 41.5 %collective-permute-start.3 = (f32[2,58,8,128]{3,2,1,0:T(8,128)}, f32[2,58,8,128]{3,2,1,0:T(8,128)S(1)}, u32[]{:S(2)}, u32[]{:S(2)}) collective-permute-start(f32[2,58,8,128]{3,2,1,0:T(8,128)} %get-tuple-element.19), channel_id=1, source_target_pairs={{1,0},{2,1},{3,2},{0,3},{5,4},{6,5},{7,6},{4,7},{9,8},{10,9},{11,1... | collective-permute-start | bytes 1425416 | tf_op jit(solution)/shard_map/ppermute | solution.py:253

commit v2 on v0

v2 whole, which is shorter than its diff:
```python
import functools

import jax
import jax.numpy as jnp
from jax import lax
from jax.experimental import pallas as pl
from jax.experimental.pallas import tpu as pltpu
from jax.sharding import PartitionSpec as P

STEPS = 8
DEPTH = 4
LANES = 128
TOP = 8
MESH = pl.DeviceIdType.MESH
HIGHEST = lax.Precision.HIGHEST

diffuse_x = 0.25
diffuse_z = 0.2
sat_scale = 0.5
sat_slope = 0.3
cond_rate = 0.5
latent_gain = 0.4
LOG2E = 1.4426950408889634


def round_up(n, m):
    return -(-n // m) * m


def contract(a, b, dims):
    return lax.dot_general(
        a, b, (dims, ((), ())), precision=HIGHEST, preferred_element_type=jnp.float32
    )


def window_kernel(
    depth,
    prof_ref,
    cour_ref,
    owner_ref,
    cloud_ref,
    x_ref,
    tend_ref,
    final_ref,
    xs,
    outs,
    buf,
    sends,
    gets,
    give,
    take,
    fsend,
    fland,
    force,
    wind,
    part,
    heap,
    mine,
    inc,
    pack,
    land,
    local_sem,
    halo_sem,
    force_sem,
    sum_sem,
    back_sem,
):
    fields, levels, cells = xs.shape[1:4]
    chunks = xs.shape[0]
    groups, cap = fland.shape[:2]
    columns = owner_ref.shape[1]
    peers = lax.axis_size("grp")
    z_me = lax.axis_index("grp")
    c_me = lax.axis_index("col")
    rounds = STEPS // depth
    width = cells + 2 * depth
    span = lambda i: pl.ds(i * LANES, LANES)

    loads = []
    for c in range(chunks):
        load = pltpu.make_async_copy(
            x_ref.at[:, :, :, span(c)], xs.at[c], local_sem.at[0, c]
        )
        load.start()
        loads.append(load)

    barrier = pltpu.get_barrier_semaphore()
    for k in range(1, peers):
        pl.semaphore_signal(
            barrier, inc=1, device_id={"grp": lax.rem(z_me + k, peers)}, device_id_type=MESH
        )
    for k in range(1, groups):
        pl.semaphore_signal(
            barrier, inc=1, device_id={"col": lax.rem(c_me + k, groups)}, device_id_type=MESH
        )

    def halo_copies(c, r):
        copies = []
        for side in range(2):
            peer = lax.rem(z_me + (peers - 1 if side == 0 else 1), peers)
            copies.append(
                pltpu.make_async_remote_copy(
                    src_ref=sends.at[c, r, side],
                    dst_ref=gets.at[c, r, side],
                    send_sem=halo_sem.at[0, c, r, side],
                    recv_sem=halo_sem.at[1, c, r, side],
                    device_id={"grp": peer},
                    device_id_type=MESH,
                )
            )
        return copies

    waits = []
    for c in range(chunks):
        loads[c].wait()

        def fill(z, carry):
            for f in range(fields):
                x = xs[c, f, z]
                buf[c, 0, f, z, TOP : TOP + cells] = x
                sends[c, 0, 0, f, z] = x[:depth]
                sends[c, 0, 1, f, z] = x[cells - depth :]
            return carry

        lax.fori_loop(0, levels, fill, 0)
        if c == 0:
            pl.semaphore_wait(barrier, peers - 1 + groups - 1)
        for copy in halo_copies(c, 0):
            copy.start()
            waits.append(copy)

    owner = owner_ref[...]
    own_row = owner_ref[pl.ds(c_me, 1), :]
    group_ids = lax.broadcasted_iota(jnp.int32, (groups, columns), 0)
    earlier = (
        lax.broadcasted_iota(jnp.int32, (columns, columns), 0)
        < lax.broadcasted_iota(jnp.int32, (columns, columns), 1)
    ).astype(jnp.float32)
    slot = lax.broadcasted_iota(jnp.int32, (cap, columns), 0).astype(jnp.float32)
    spot = lax.broadcasted_iota(jnp.int32, (cap, columns), 1).astype(jnp.float32) + 1.0

    def ranked(hits):
        rank = jnp.dot(hits, earlier, preferred_element_type=jnp.float32)
        return jnp.where(hits > 0.5, rank, -1.0)

    low = own_row - group_ids * columns
    order = ranked(jnp.where((low >= 0) & (low < columns), 1.0, 0.0))
    for q in range(groups):
        give[q * cap : (q + 1) * cap, :] = jnp.where(order[q : q + 1] == slot, 1.0, 0.0)

    for f, ref in ((0, prof_ref), (1, cour_ref)):
        lines = ref.shape[0]
        fsend[:, :, f * LANES : f * LANES + lines] = contract(
            give[...], ref[...], ((1,), (1,))
        ).reshape(groups, cap, lines)
    shares = []
    for k in range(1, groups):
        peer = lax.rem(c_me + k, groups)
        copy = pltpu.make_async_remote_copy(
            src_ref=fsend.at[peer],
            dst_ref=fland.at[c_me],
            send_sem=force_sem.at[0, k],
            recv_sem=force_sem.at[1, k],
            device_id={"col": peer},
            device_id_type=MESH,
        )
        copy.start()
        shares.append(copy)
    waits += shares
    fland[c_me] = fsend[c_me]

    local = owner - c_me * columns
    order = ranked(jnp.where((local >= 0) & (local < columns), 1.0, 0.0))
    place = (local + 1).astype(jnp.float32)
    for q in range(groups):
        chosen = jnp.where(order[q : q + 1] == slot, place[q : q + 1], 0.0)
        chosen = jnp.sum(chosen, axis=1, keepdims=True)
        take[q * cap : (q + 1) * cap, :] = jnp.where(chosen == spot, 1.0, 0.0)

    for copy in shares:
        copy.wait_recv()
    phys = contract(
        fland[:, :, :LANES].reshape(groups * cap, LANES), take[...], ((0,), (0,))
    )
    for f in range(fields):
        for c in range(chunks):
            force[c, f] = (
                phys[f * levels : (f + 1) * levels, c * LANES : (c + 1) * LANES] / STEPS
            )
    phys = contract(
        fland[:, :, LANES:].reshape(groups * cap, LANES), take[...], ((0,), (0,))
    )
    for c in range(chunks):
        wind[c] = phys[:levels, c * LANES : (c + 1) * LANES]
    half_cloud = cond_rate * cloud_ref[...].astype(jnp.float32)

    def stepped(c, src, z, count):
        up = jnp.minimum(z + 1, levels - 1)
        down = jnp.maximum(z - 1, 0)
        lanes = slice(c * LANES, (c + 1) * LANES)
        speed = 0.5 * wind[c, pl.ds(z, 1), :]
        new = []
        for f in range(fields):
            here = buf[c, src, f, z, TOP : TOP + count]
            west = buf[c, src, f, z, TOP - 1 : TOP - 1 + count]
            east = buf[c, src, f, z, TOP + 1 : TOP + 1 + count]
            upper = buf[c, src, f, up, TOP : TOP + count]
            lower = buf[c, src, f, down, TOP : TOP + count]
            new.append(
                (1.0 - 2.0 * diffuse_x - 2.0 * diffuse_z) * here
                + ((diffuse_x + speed) * west + (diffuse_x - speed) * east)
                + (diffuse_z * (upper + lower) + force[c, f, pl.ds(z, 1), :])
            )
        energy, moisture = new
        excess = (moisture + sat_scale) - sat_scale * jnp.exp2((sat_slope * LOG2E) * energy)
        amount = jnp.maximum(excess, 0.0) * half_cloud[:, lanes]
        return energy + latent_gain * amount, moisture - amount

    def sweep(c, src):
        def level(z, carry):
            for f, value in enumerate(stepped(c, src, z, width)):
                buf[c, 1 - src, f, z, TOP : TOP + width] = value
                buf[c, 1 - src, f, z, TOP - 1 : TOP] = value[width - 1 :]
                buf[c, 1 - src, f, z, TOP + width : TOP + width + 1] = value[:1]
            return carry

        lax.fori_loop(0, levels, level, 0, unroll=2)

    def last(c, src):
        def level(z, carry):
            for f, value in enumerate(stepped(c, src, z, cells)):
                outs[c, f, z] = value
                part[c, pl.ds(f * levels + z, 1), :] = jnp.sum(
                    value - xs[c, f, z], axis=0, keepdims=True
                )
            return carry

        lax.fori_loop(0, levels, level, 0, unroll=2)

    lines = part.shape[1] // peers
    block = lambda i: pl.ds(pl.multiple_of(i * lines, lines), lines)

    def sum_copies(c, phase):
        copies = []
        for k in range(1, peers):
            peer = lax.rem(z_me + k, peers)
            if phase == 0:
                source, target = part.at[c, block(peer)], heap.at[c, k]
            else:
                source, target = mine.at[c], inc.at[c, block(z_me)]
            copies.append(
                pltpu.make_async_remote_copy(
                    src_ref=source,
                    dst_ref=target,
                    send_sem=sum_sem.at[phase, 0, c, k],
                    recv_sem=sum_sem.at[phase, 1, c, k],
                    device_id={"grp": peer},
                    device_id_type=MESH,
                )
            )
        for copy in copies:
            copy.start()
            waits.append(copy)
        return copies

    def add_up(c, scatter):
        total = part[c, block(z_me), :]
        for k, copy in enumerate(scatter):
            copy.wait_recv()
            total = total + heap[c, k + 1]
        total = total / (cells * peers)
        mine[c] = total
        inc[c, block(z_me), :] = total
        return sum_copies(c, 1)

    pad_rows = part.shape[1] - fields * levels
    if pad_rows:
        for c in range(chunks):
            part[c, fields * levels :, :] = jnp.zeros((pad_rows, LANES), jnp.float32)

    scatters, gathers, stores = [], [], []
    for r in range(rounds):
        for c in range(chunks):
            for copy in halo_copies(c, r):
                copy.wait_recv()
            src = (r * depth) % 2

            def widen(z, carry):
                for f in range(fields):
                    right = gets[c, r, 0, f, z]
                    left = gets[c, r, 1, f, z]
                    buf[c, src, f, z, TOP + cells : TOP + cells + depth] = right
                    buf[c, src, f, z, TOP + cells + depth : TOP + width] = left
                    buf[c, src, f, z, TOP - 1 : TOP] = left[depth - 1 :]
                    buf[c, src, f, z, TOP + width : TOP + width + 1] = buf[
                        c, src, f, z, TOP : TOP + 1
                    ]
                return carry

            lax.fori_loop(0, levels, widen, 0)
            final_round = r == rounds - 1
            if final_round and c > 0:
                gathers += add_up(c - 1, scatters[c - 1])
            for s in range(depth - 1 if final_round else depth):
                sweep(c, (src + s) % 2)
            src = (src + depth - (1 if final_round else 0)) % 2
            if not final_round:

                def narrow(z, carry):
                    for f in range(fields):
                        sends[c, r + 1, 0, f, z] = buf[c, src, f, z, TOP : TOP + depth]
                        sends[c, r + 1, 1, f, z] = buf[
                            c, src, f, z, TOP + cells - depth : TOP + cells
                        ]
                    return carry

                lax.fori_loop(0, levels, narrow, 0)
                for copy in halo_copies(c, r + 1):
                    copy.start()
                    waits.append(copy)
            else:
                last(c, src)
                scatters.append(sum_copies(c, 0))
                store = pltpu.make_async_copy(
                    outs.at[c], final_ref.at[:, :, :, span(c)], local_sem.at[1, c]
                )
                store.start()
                stores.append(store)
    gathers += add_up(chunks - 1, scatters[chunks - 1])
    for copy in gathers:
        copy.wait_recv()
    packed = 0.0
    for c in range(chunks):
        packed = packed + contract(
            take[:, c * LANES : (c + 1) * LANES], inc[c], ((1,), (1,))
        )
    pack[...] = packed.reshape(pack.shape)
    returns = []
    for k in range(1, groups):
        peer = lax.rem(c_me + k, groups)
        copy = pltpu.make_async_remote_copy(
            src_ref=pack.at[peer],
            dst_ref=land.at[c_me],
            send_sem=back_sem.at[0, k],
            recv_sem=back_sem.at[1, k],
            device_id={"col": peer},
            device_id_type=MESH,
        )
        copy.start()
        returns.append(copy)
    waits += returns
    land[c_me] = pack[c_me]
    for copy in returns:
        copy.wait_recv()
    back = contract(land[...].reshape(groups * cap, land.shape[2]), give[...], ((0,), (0,)))
    tend_ref[...] = back[: fields * levels]
    for copy in waits:
        copy.wait_send()
    for store in stores:
        store.wait()


def on_device(profiles, courant, owner_map, cloud_flags, crm_state):
    columns = profiles.shape[0]
    fields, levels, cells = crm_state.shape[:3]
    groups = lax.axis_size("col")
    peers = lax.axis_size("grp")
    per_peer = columns // groups
    cap = round_up(per_peer + min(2, per_peer), 8)
    chunks = columns // LANES
    depth = min(DEPTH, cells)
    rounds = STEPS // depth
    rows = round_up(fields * levels, 8 * peers)
    wide = round_up(rows, LANES)
    f32 = lambda *shape: pltpu.VMEM(shape, jnp.float32)
    dma = lambda *shape: pltpu.SemaphoreType.DMA(shape)
    vmem = pl.BlockSpec(memory_space=pltpu.VMEM)
    anywhere = pl.BlockSpec(memory_space=pl.ANY)
    tall = round_up(TOP + cells + 2 * depth + 1, 8)
    tendency, final = pl.pallas_call(
        functools.partial(window_kernel, depth),
        out_shape=(
            jax.ShapeDtypeStruct((fields * levels, columns), jnp.float32),
            jax.ShapeDtypeStruct(crm_state.shape, jnp.float32),
        ),
        in_specs=[vmem, vmem, vmem, vmem, anywhere],
        out_specs=(vmem, anywhere),
        scratch_shapes=[
            f32(chunks, fields, levels, cells, LANES),
            f32(chunks, fields, levels, cells, LANES),
            f32(chunks, 2, fields, levels, tall, LANES),
            f32(chunks, rounds, 2, fields, levels, depth, LANES),
            f32(chunks, rounds, 2, fields, levels, depth, LANES),
            f32(groups * cap, columns),
            f32(groups * cap, columns),
            f32(groups, cap, 2 * LANES),
            f32(groups, cap, 2 * LANES),
            f32(chunks, fields, levels, LANES),
            f32(chunks, levels, LANES),
            f32(chunks, rows, LANES),
            f32(chunks, peers, rows // peers, LANES),
            f32(chunks, rows // peers, LANES),
            f32(chunks, rows, LANES),
            f32(groups, cap, rows),
            f32(groups, cap, rows),
            dma(2, chunks),
            dma(2, chunks, rounds, 2),
            dma(2, groups),
            dma(2, 2, chunks, peers),
            dma(2, groups),
        ],
        compiler_params=pltpu.CompilerParams(
            collective_id=0, has_side_effects=True, vmem_limit_bytes=56 * 2**20
        ),
    )(profiles.T, courant.T, owner_map.reshape(groups, columns), cloud_flags[None, :], crm_state)
    return tendency.T, final


def solution(mesh):
    placed = (P("col", None), P("col", None), P(), P("col"), P(None, None, "grp", "col"))
    return jax.shard_map(
        on_device,
        mesh=mesh,
        in_specs=placed,
        out_specs=(P("col", None), P(None, None, "grp", "col")),
        check_vma=False,
    )
```

time: 159 us -> 76.9 us (0.48)
  Pallas kernels: 0 us -> 70.2 us
  waiting for transfers between devices: 68.8 us -> 0 us
  starting transfers between devices: 28.6 us -> 0 us
  other arithmetic: 28 us -> 0 us
  between operations: 14.7 us -> 0.64 us
  local copies, waits for them, and re-layouts: 18.8 us -> 5.78 us
    pallas_call x0 -> x1, Pallas kernels: none -> 70.2 us  [on_device(): pl.pallas_call(functools.partial(window_kernel, depth), out_shape=(jax.Sh...]
    psum x1 -> x0, waiting for transfers between devices: 33.6 us -> none  [on_device(): totals = lax.psum(partial_value, 'grp')]
    ppermute x8 -> x0, waiting for transfers between devices: 28.1 us -> none  [the longest x4 19.6 us: padded(): before = lax.ppermute(last, axis, up)]
    add x16 -> x0, other arithmetic: 17.2 us -> none  [the longest x8 14.8 us: advance(): centre + courant_here * ((western - eastern) * 0.5)]
    ppermute x8 -> x0, starting transfers between devices: 15.6 us -> none  [the longest x4 11.3 us: padded(): after = lax.ppermute(leading, axis, down)]
    all_to_all x3 -> x0, starting transfers between devices: 13 us -> none  [the longest x1 5.2 us: on_device(): lax.all_to_all(out_cour, 'col', split_axis=0, concat_axis=0, tiled=True)]
    all_to_all x3 -> x0, waiting for transfers between devices: 7 us -> none  [the longest x1 3.51 us: on_device(): lax.all_to_all(out_prof, 'col', split_axis=0, concat_axis=0, tiled=True)]
    gather x6 -> x0, local copies, waits for them, and re-layouts: 4.4 us -> none  [the longest x1 1.05 us: on_device(): out_cour = padded_cour[send_rows].reshape(col_count, capacity, levels)]
  transfers between devices with their start and end apart: 12 -> 0, of which waited for: 9 -> 0; matrix products, arithmetic and copies ran while one was open for 8% -> 0% of each run, Pallas kernels for 0% -> 0%
where the time goes in v2:
time: 76.9 us; the launch traced here: 76.6 us
  Pallas kernels  70.2 us (91%)
  local copies, waits for them, and re-layouts  5.78 us (8%)
    pallas_call x1, Pallas kernels, on_device(): pl.pallas_call(functools.partial(window_kernel, depth), out_shape=(jax.Sh...  70.2 us
    unnamed x2, local copies, waits for them, and re-layouts  4.48 us

profile of v2, /device:TPU:0, one launch (start us, length us, event | category | flops | bytes accessed | tf_op | source)
XLA Modules:
  0.0 76.6 jit_solution(9566849233875477750)
XLA Ops:
  0.6 1.3 %reshape.7.owner_ref = s32[8,256]{1,0:T(8,128)} reshape(s32[2048]{0:T(1024)} %param.7) | data formatting | bytes 16384 | tf_op jit(solution)/shard_map/reshape | solution.py:415
  1.9 70.2 %shard_map.68 = (f32[116,256]{1,0:T(8,128)}, f32[2,58,16,256]{3,2,1,0:T(8,128)}) custom-call(f32[116,256]{1,0:T(8,128)} %bitcast.5, f32[58,256]{1,0:T(8,128)} %bitcast.6, s32[8,256]{1,0:T(8,128)} %reshape.7.owner_ref, s32[1,256]{1,0:T(1,128)} %bitcast.7, f32[2,58,16,256]{3,2,1,0:T(8,128)} %x_ref.1), custom_call_target="tpu_custom_call" | custom-call | tf_op jit(solution)/shard_map/pallas_call | solution.py:380
  72.2 1.6 %copy.9 = f32[256,116]{0,1:T(8,128)} copy(f32[256,116]{0,1:T(8,128)} %bitcast.4) | data formatting | bytes 237568
  73.7 2.9 %copy.10 = f32[2,58,16,256]{3,2,1,0:T(8,128)} copy(f32[2,58,16,256]{3,2,1,0:T(8,128)} %get-tuple-element.9) | data formatting | bytes 3801088

commit v3 on v2

--- a/solution.py
+++ b/solution.py
@@ -10,6 +10,7 @@
 STEPS = 8
 DEPTH = 4
 LANES = 128
+LIMIT = 36 * 2**20
 TOP = 8
 MESH = pl.DeviceIdType.MESH
 HIGHEST = lax.Precision.HIGHEST
@@ -40,14 +41,14 @@
     owner_ref,
     cloud_ref,
     x_ref,
-    tend_ref,
+    land,
+    give,
     final_ref,
     xs,
     outs,
     buf,
     sends,
     gets,
-    give,
     take,
     fsend,
     fland,
@@ -58,7 +59,6 @@
     mine,
     inc,
     pack,
-    land,
     local_sem,
     halo_sem,
     force_sem,
@@ -68,7 +68,7 @@
     fields, levels, cells = xs.shape[1:4]
     chunks = xs.shape[0]
     groups, cap = fland.shape[:2]
-    columns = owner_ref.shape[1]
+    columns = chunks * LANES
     peers = lax.axis_size("grp")
     z_me = lax.axis_index("grp")
     c_me = lax.axis_index("col")
@@ -129,8 +129,12 @@
             copy.start()
             waits.append(copy)
 
-    owner = owner_ref[...]
-    own_row = owner_ref[pl.ds(c_me, 1), :]
+    owner = jnp.concatenate(
+        [owner_ref[pl.ds(c, groups, stride=chunks), :] for c in range(chunks)], axis=1
+    )
+    own_row = jnp.concatenate(
+        [owner_ref[pl.ds(c_me * chunks + c, 1), :] for c in range(chunks)], axis=1
+    )
     group_ids = lax.broadcasted_iota(jnp.int32, (groups, columns), 0)
     earlier = (
         lax.broadcasted_iota(jnp.int32, (columns, columns), 0)
@@ -352,12 +356,24 @@
     land[c_me] = pack[c_me]
     for copy in returns:
         copy.wait_recv()
-    back = contract(land[...].reshape(groups * cap, land.shape[2]), give[...], ((0,), (0,)))
-    tend_ref[...] = back[: fields * levels]
     for copy in waits:
         copy.wait_send()
     for store in stores:
         store.wait()
+
+
+def finish_kernel(land_ref, give_ref, state_ref, tend_ref, final_ref, sems):
+    fields = state_ref.shape[0]
+    store = [
+        pltpu.make_async_copy(state_ref.at[f], final_ref.at[f], sems.at[f]) for f in range(fields)
+    ]
+    for copy in store:
+        copy.start()
+    groups, cap, rows = land_ref.shape
+    back = contract(land_ref[...].reshape(groups * cap, rows), give_ref[...], ((0,), (0,)))
+    tend_ref[...] = back[: tend_ref.shape[0]]
+    for copy in store:
+        copy.wait()
 
 
 def on_device(profiles, courant, owner_map, cloud_flags, crm_state):
@@ -371,27 +387,26 @@
     depth = min(DEPTH, cells)
     rounds = STEPS // depth
     rows = round_up(fields * levels, 8 * peers)
-    wide = round_up(rows, LANES)
     f32 = lambda *shape: pltpu.VMEM(shape, jnp.float32)
     dma = lambda *shape: pltpu.SemaphoreType.DMA(shape)
     vmem = pl.BlockSpec(memory_space=pltpu.VMEM)
     anywhere = pl.BlockSpec(memory_space=pl.ANY)
     tall = round_up(TOP + cells + 2 * depth + 1, 8)
-    tendency, final = pl.pallas_call(
+    land, give, state = pl.pallas_call(
         functools.partial(window_kernel, depth),
         out_shape=(
-            jax.ShapeDtypeStruct((fields * levels, columns), jnp.float32),
+            jax.ShapeDtypeStruct((groups, cap, rows), jnp.float32),
+            jax.ShapeDtypeStruct((groups * cap, columns), jnp.float32),
             jax.ShapeDtypeStruct(crm_state.shape, jnp.float32),
         ),
-        in_specs=[vmem, vmem, vmem, vmem, anywhere],
-        out_specs=(vmem, anywhere),
+        in_specs=[vmem, vmem, vmem, vmem, pl.BlockSpec(memory_space=pltpu.HBM)],
+        out_specs=(vmem, vmem, anywhere),
         scratch_shapes=[
             f32(chunks, fields, levels, cells, LANES),
             f32(chunks, fields, levels, cells, LANES),
             f32(chunks, 2, fields, levels, tall, LANES),
             f32(chunks, rounds, 2, fields, levels, depth, LANES),
             f32(chunks, rounds, 2, fields, levels, depth, LANES),
-            f32(groups * cap, columns),
             f32(groups * cap, columns),
             f32(groups, cap, 2 * LANES),
             f32(groups, cap, 2 * LANES),
@@ -402,7 +417,6 @@
             f32(chunks, rows // peers, LANES),
             f32(chunks, rows, LANES),
             f32(groups, cap, rows),
-            f32(groups, cap, rows),
             dma(2, chunks),
             dma(2, chunks, rounds, 2),
             dma(2, groups),
@@ -410,9 +424,26 @@
             dma(2, groups),
         ],
         compiler_params=pltpu.CompilerParams(
-            collective_id=0, has_side_effects=True, vmem_limit_bytes=56 * 2**20
+            collective_id=0, has_side_effects=True, vmem_limit_bytes=LIMIT
         ),
-    )(profiles.T, courant.T, owner_map.reshape(groups, columns), cloud_flags[None, :], crm_state)
+    )(
+        profiles.T,
+        courant.T,
+        owner_map.reshape(groups * chunks, LANES),
+        cloud_flags[None, :],
+        crm_state,
+    )
+    tendency, final = pl.pallas_call(
+        finish_kernel,
+        out_shape=(
+            jax.ShapeDtypeStruct((fields * levels, columns), jnp.float32),
+            jax.ShapeDtypeStruct(crm_state.shape, jnp.float32),
+        ),
+        in_specs=[vmem, vmem, anywhere],
+        out_specs=(vmem, anywhere),
+        scratch_shapes=[dma(fields)],
+        compiler_params=pltpu.CompilerParams(vmem_limit_bytes=4 * 2**20),
+    )(land, give, state)
     return tendency.T, final
 
 

time: 76.9 us -> 75.4 us (0.980)
  local copies, waits for them, and re-layouts: 5.78 us -> 4.63 us
    pallas_call x1, Pallas kernels: 70.2 us -> 67.9 us  [on_device(): pl.pallas_call(functools.partial(window_kernel, depth), out_shape=(jax.Sh...]
    pallas_call x0 -> x1, Pallas kernels: none -> 1.93 us  [on_device(): pl.pallas_call(finish_kernel, out_shape=(jax.ShapeDtypeStruct((fields * l...]
    reshape x1 -> x0, local copies, waits for them, and re-layouts: 1.3 us -> none  [on_device(): owner_map.reshape(groups, columns)]
    unnamed x2 -> x10, local copies, waits for them, and re-layouts: 4.48 us -> 4.63 us
where the time goes in v3:
time: 75.4 us; the launch traced here: 75.1 us
  Pallas kernels  69.9 us (93%)
  local copies, waits for them, and re-layouts  4.63 us (6%)
    pallas_call x1, Pallas kernels, on_device(): pl.pallas_call(functools.partial(window_kernel, depth), out_shape=(jax.Sh...  67.9 us
    unnamed x10, local copies, waits for them, and re-layouts  4.63 us
    pallas_call x1, Pallas kernels, on_device(): pl.pallas_call(finish_kernel, out_shape=(jax.ShapeDtypeStruct((fields * l...  1.93 us

profile of v3, /device:TPU:0, one launch (start us, length us, event | category | flops | bytes accessed | tf_op | source)
XLA Modules:
  0.0 75.1 jit_solution(7285671973907305929)
XLA Ops:
  0.6 0.0 copy-start
  0.6 1.5 %copy-done = f32[2,58,16,256]{3,2,1,0:T(8,128)S(1)} copy-done((f32[2,58,16,256]{3,2,1,0:T(8,128)S(1)}, f32[2,58,16,256]{3,2,1,0:T(8,128)}, u32[]{:S(2)}) %copy-start) | copy-done | bytes 1900568
  2.2 0.0 copy-start.1
  2.2 0.9 %copy-done.1 = f32[256,116]{0,1:T(8,128)S(1)} copy-done((f32[256,116]{0,1:T(8,128)S(1)}, f32[256,116]{0,1:T(8,128)}, u32[]{:S(2)}) %copy-start.1) | copy-done | bytes 118808
  3.1 0.0 copy-start.2
  3.1 0.8 %copy-done.2 = f32[256,58]{0,1:T(8,128)S(1)} copy-done((f32[256,58]{0,1:T(8,128)S(1)}, f32[256,58]{0,1:T(8,128)}, u32[]{:S(2)}) %copy-start.2) | copy-done | bytes 59416
  3.9 0.0 copy-start.3
  3.9 0.7 copy-done.3
  4.6 0.0 copy-start.4
  4.6 0.7 copy-done.4
  5.3 67.9 %shard_map.68 = (f32[8,40,128]{2,1,0:T(8,128)S(1)}, f32[320,256]{1,0:T(8,128)S(1)}, f32[2,58,16,256]{3,2,1,0:T(8,128)S(1)}) custom-call(f32[116,256]{1,0:T(8,128)S(1)} %bitcast.5, f32[58,256]{1,0:T(8,128)S(1)} %bitcast.6, s32[16,128]{1,0:T(8,128)S(1)} %bitcast.7, s32[1,256]{1,0:T(1,128)S(1)} %bitcast.8, f32[2,58,16,256]{3,2,1,0:T(8,128)S(1)} %copy-done), custom_call_target="tpu_custom_call" | custom-call | tf_op jit(solution)/shard_map/pallas_call | solution.py:395
  73.2 1.9 %shard_map.69 = (f32[116,256]{1,0:T(8,128)}, f32[2,58,16,256]{3,2,1,0:T(8,128)}) custom-call(f32[8,40,128]{2,1,0:T(8,128)S(1)} %get-tuple-element.7.land_ref, f32[320,256]{1,0:T(8,128)S(1)} %get-tuple-element.8.give_ref, f32[2,58,16,256]{3,2,1,0:T(8,128)S(1)} %get-tuple-element.9.state_ref), custom_call_target="tpu_custom_call" | custom-call | tf_op jit(solution)/shard_map/pallas_call | solution.py:436
Async XLA Ops:
  0.6 1.5 %copy-start = (f32[2,58,16,256]{3,2,1,0:T(8,128)S(1)}, f32[2,58,16,256]{3,2,1,0:T(8,128)}, u32[]{:S(2)}) copy-start(f32[2,58,16,256]{3,2,1,0:T(8,128)} %x_ref.1) | copy-start | bytes 5701636
  2.2 0.9 %copy-start.1 = (f32[256,116]{0,1:T(8,128)S(1)}, f32[256,116]{0,1:T(8,128)}, u32[]{:S(2)}) copy-start(f32[256,116]{0,1:T(8,128)} %param.5) | copy-start | bytes 356356
  3.1 0.8 %copy-start.2 = (f32[256,58]{0,1:T(8,128)S(1)}, f32[256,58]{0,1:T(8,128)}, u32[]{:S(2)}) copy-start(f32[256,58]{0,1:T(8,128)} %param.6) | copy-start | bytes 178180
  3.9 0.7 copy-start.3
  4.6 0.7 copy-start.4
